TPU v7x, 32 devices: a whole 2x2x4 slice. The times are simulated.
32 devices in a mesh: px: 8 (over y, x, core), py: 4 (over z).
Axes of the slice: x: 2, y: 2, z: 4, core: 2. Of those that a mesh axis runs over, the one named last changes fastest.
Arguments:
- source: float32 [1024, 512, 128], P('px', 'py'), may hold values from -8 to 8
- layer_mass: float32 [128], replicated, may hold values from 0.5 to 4
- modes: float32 [128, 128], replicated, may hold values from -0.5 to 0.5
- mode_eigen: float32 [128], replicated, may hold values from 0.0002 to 1
Outputs:
- solution: float32 [1024, 512, 128], P('px', 'py')
All inputs are finite; a program needn't handle non-finite values.
Results may differ from a plain program's by a relative error of at most 0.0014.
Values sent between devices are 32-bit elements; how exact they have to be, the bound alone decides.
A program may use at most 128 MiB of HBM per device.

v0:
```python
import jax
import jax.numpy as jnp
from jax import lax
from jax.sharding import PartitionSpec as P

NX = 1024
NY = 512


def cosine_table(length):
    rows = jnp.arange(length, dtype=jnp.float32)[:, None]
    cols = jnp.arange(length, dtype=jnp.float32)[None, :]
    scale = jnp.where(rows == 0.0, jnp.sqrt(1.0 / length), jnp.sqrt(2.0 / length)).astype(
        jnp.float32
    )
    return scale * jnp.cos(jnp.pi * (cols + 0.5) * rows / length)


def laplace_eigen(length):
    waves = jnp.arange(length, dtype=jnp.float32)
    return 2.0 - 2.0 * jnp.cos(jnp.pi * waves / length)


def shards(source, layer_mass, modes, mode_eigen):
    high = lax.Precision.HIGHEST
    rows_x, rows_y, levels = source.shape
    count_x = lax.axis_size("px")
    count_y = lax.axis_size("py")
    table_x = cosine_table(NX)
    table_y = cosine_table(NY)
    wave_x = laplace_eigen(NX)
    wave_y = laplace_eigen(NY)
    weighted = source * layer_mass
    modal_field = jnp.einsum("xyz,zk->kxy", weighted, modes, precision=high)
    devices = count_x * count_y
    group = levels // devices
    sent = modal_field.reshape(levels, 1, rows_x, rows_y)
    arrived = lax.all_to_all(sent, ("px", "py"), split_axis=0, concat_axis=1, tiled=True)
    planes = arrived.reshape(group, count_x, count_y, rows_x, rows_y)
    planes = planes.transpose(0, 1, 3, 2, 4).reshape(group, NX, NY)
    first_mode = (lax.axis_index("px") * count_y + lax.axis_index("py")) * group
    eigen_part = lax.dynamic_slice_in_dim(mode_eigen, first_mode, group)
    spectral = jnp.einsum("ax,kxy->kay", table_x, planes, precision=high)
    spectral = jnp.einsum("kxb,ab->kxa", spectral, table_y, precision=high)
    scaled = spectral / (eigen_part[:, None, None] + wave_x[None, :, None] + wave_y[None, None, :])
    returned = jnp.einsum("kxa,ab->kxb", scaled, table_y, precision=high)
    returned = jnp.einsum("ax,kay->kxy", table_x, returned, precision=high)
    outgoing = returned.reshape(group, count_x, rows_x, count_y, rows_y)
    outgoing = outgoing.transpose(0, 1, 3, 2, 4).reshape(group, devices, rows_x, rows_y)
    gathered = lax.all_to_all(outgoing, ("px", "py"), split_axis=1, concat_axis=0, tiled=True)
    gathered = gathered.reshape(levels, rows_x, rows_y)
    return jnp.einsum("kxy,zk->xyz", gathered, modes, precision=high)


def solution(mesh):
    placed = (P("px", "py", None), P(), P(), P())
    return jax.shard_map(
        shards, mesh=mesh, in_specs=placed, out_specs=P("px", "py", None), check_vma=False
    )
```

profile of v0, /device:TPU:0, one launch (start us, length us, event | category | flops | bytes accessed | tf_op | source)
XLA Modules:
  0.0 588.8 jit_solution(6842478408248113124)
XLA Ops:
  0.0 0.0 copy-start
  0.0 0.8 copy-done
  0.8 10.8 %fusion.16 = f32[128,1,128,128]{0,3,2,1:T(8,128)} fusion(f32[128,128,128]{2,1,0:T(8,128)} %param.4, f32[128]{0:T(128)} %param.5, f32[128,128]{1,0:T(8,128)S(1)} %copy-done), kind=kOutput, calls=%fused_computation.17 | convolution fusion | flops 3223322624 | bytes 16843264 | tf_op jit(solution)/shard_map/xyz,zk->kxy/dot_general | solution.py:34
  11.7 9.3 %copy.10 = f32[128,1,128,128]{3,2,1,0:T(8,128)} copy(f32[128,1,128,128]{0,3,2,1:T(8,128)} %fusion.16) | data formatting | bytes 16777216 | tf_op jit(solution)/shard_map/reshape | solution.py:37
  21.0 7.8 %all-to-all-start = ((f32[128,1,128,128]{3,2,1,0:T(8,128)}), f32[128,1,128,128]{3,2,1,0:T(8,128)}, u32[]{:S(2)}, u32[]{:S(2)}) async-start(f32[128,1,128,128]{3,2,1,0:T(8,128)} %copy.10), calls=%async_computation | async-start | bytes 16777216 | tf_op jit(solution)/shard_map/all_to_all | solution.py:38
  28.8 0.0 copy-done.2
  28.8 0.1 dynamic_slice.3
  29.0 0.1 broadcast_add_fusion
  29.1 15.0 %fusion.51 = f32[1024,1024,1]{1,0,2:T(8,128)} fusion(f32[1024]{0:T(1024)S(1)} %get-tuple-element.5, f32[1024]{0:T(1024)S(1)} %get-tuple-element.6), kind=kLoop, calls=%fused_computation.12.clone.1 | loop fusion | flops 3145728 | bytes 4202496 | tf_op jit(solution)/shard_map/ax,kxy->kay/dot_general | solution.py:43
  44.1 14.9 %fusion.49 = f32[1024,1024,1]{1,0,2:T(8,128)} fusion(f32[1024]{0:T(1024)S(1)} %get-tuple-element.5, f32[1024]{0:T(1024)S(1)} %get-tuple-element.6), kind=kLoop, calls=%fused_computation.10.clone.1 | loop fusion | flops 3145728 | bytes 4202496 | tf_op jit(solution)/shard_map/ax,kay->kxy/dot_general | solution.py:47
  59.0 151.2 %all-to-all-done = f32[128,1,128,128]{3,2,1,0:T(8,128)} async-done(((f32[128,1,128,128]{3,2,1,0:T(8,128)}), f32[128,1,128,128]{3,2,1,0:T(8,128)}, u32[]{:S(2)}, u32[]{:S(2)}) %all-to-all-start) | async-done | bytes 8388640 | tf_op jit(solution)/shard_map/all_to_all | solution.py:38
  210.2 9.9 %copy.11 = f32[4,8,4,128,128]{3,1,4,2,0:T(8,128)} copy(f32[4,8,4,128,128]{4,3,0,2,1:T(8,128)} %bitcast.5) | data formatting | bytes 16777216 | tf_op jit(solution)/shard_map/reshape | solution.py:39
  220.1 9.3 %reshape.98 = f32[4,1024,512]{1,2,0:T(8,128)} reshape(f32[4,8,128,4,128]{2,1,4,3,0:T(8,128)} %bitcast.60) | data formatting | bytes 16777216 | tf_op jit(solution)/shard_map/reshape | solution.py:40
  229.4 30.5 %fusion.11 = f32[4,512,1024]{2,1,0:T(8,128)S(1)} fusion(f32[4,1024,512]{1,2,0:T(8,128)} %reshape.98, f32[1024,1024,1]{1,0,2:T(8,128)} %fusion.51), kind=kOutput, calls=%fused_computation.11 | convolution fusion | flops 25769803776 | bytes 20971520 | tf_op jit(solution)/shard_map/ax,kxy->kay/dot_general | solution.py:43
  259.9 44.8 %fusion = f32[4,1024,512]{2,1,0:T(8,128)S(1)} fusion(f32[4,512,1024]{2,1,0:T(8,128)S(1)} %fusion.11, f32[512]{0:T(512)S(1)} %get-tuple-element.7, f32[512]{0:T(512)S(1)} %get-tuple-element.8), kind=kOutput, calls=%fused_computation | convolution fusion | flops 12885688320 | bytes 16781312 | tf_op jit(solution)/shard_map/kxb,ab->kxa/dot_general | solution.py:44
  304.7 0.0 copy-start.1
  304.7 22.3 %fusion.4 = f32[4,1024,512]{1,2,0:T(8,128)} fusion(f32[4,1024,512]{2,1,0:T(8,128)S(1)} %fusion, f32[512]{0:T(512)S(1)} %multiply_subtract_fusion.1, f32[4,1024]{1,0:T(4,128)S(1)} %broadcast_add_fusion, f32[512]{0:T(512)S(1)} %get-tuple-element.7, f32[512]{0:T(512)S(1)} %get-tuple-element.8), kind=kOutput, calls=%fused_computation.4 | convolution fusion | flops 12889882624 | bytes 16799744 | tf_op jit(solution)/shard_map/kxa,ab->kxb/dot_general | solution.py:46
  327.1 0.0 copy-done.1
  327.1 29.6 %fusion.9 = f32[4,512,1024]{2,1,0:T(8,128)S(1)} fusion(f32[4,1024,512]{1,2,0:T(8,128)} %fusion.4, f32[1024,1024,1]{1,0,2:T(8,128)S(1)} %copy-done.1), kind=kOutput, calls=%fused_computation.9 | convolution fusion | flops 25769803776 | bytes 20971520 | tf_op jit(solution)/shard_map/ax,kay->kxy/dot_general | solution.py:47
  356.7 5.5 copy.19
  362.1 9.9 %copy.14 = f32[4,8,128,4,128]{4,2,3,1,0:T(8,128)} copy(f32[4,8,128,4,128]{2,1,4,3,0:T(8,128)} %bitcast.61) | data formatting | bytes 16777216 | tf_op jit(solution)/shard_map/reshape | solution.py:48
  372.1 4.0 copy.15
  376.0 190.6 %all_to_all.30 = f32[4,32,128,128]{3,2,0,1:T(8,128)S(1)} all-to-all(f32[4,32,128,128]{3,2,0,1:T(8,128)S(1)} %copy.15), channel_id=1, replica_groups=mesh['px'=8,'py'=4] {'px','py'}, dimensions={1} | all-to-all | bytes 16777216 | tf_op jit(solution)/shard_map/all_to_all | solution.py:50
  566.7 21.9 %fusion.2 = f32[128,128,128]{2,1,0:T(8,128)} fusion(f32[128,128,128]{2,1,0:T(8,128)S(1)} %bitcast.59, f32[128,128]{1,0:T(8,128)S(1)} %copy-done), kind=kOutput, calls=%fused_computation.2 | convolution fusion | flops 3221225472 | bytes 16842752 | tf_op jit(solution)/shard_map/kxy,zk->xyz/dot_general | solution.py:52
  (5 shorter events, 0.1 us)
Async XLA Ops:
  0.0 0.8 copy-start
  21.0 7.9 %copy-start.2 = (f32[128]{0:T(128)S(1)}, f32[128]{0:T(128)}, u32[]{:S(2)}) copy-start(f32[128]{0:T(128)} %param.7) | copy-start | bytes 1540
  21.0 189.2 %all-to-all-start = ((f32[128,1,128,128]{3,2,1,0:T(8,128)}), f32[128,1,128,128]{3,2,1,0:T(8,128)}, u32[]{:S(2)}, u32[]{:S(2)}) async-start(f32[128,1,128,128]{3,2,1,0:T(8,128)} %copy.10), calls=%async_computation | async-start | bytes 16777216 | tf_op jit(solution)/shard_map/all_to_all | solution.py:38
  304.7 22.3 %copy-start.1 = (f32[1024,1024,1]{1,0,2:T(8,128)S(1)}, f32[1024,1024,1]{1,0,2:T(8,128)}, u32[]{:S(2)}) copy-start(f32[1024,1024,1]{1,0,2:T(8,128)} %fusion.49) | copy-start | bytes 12582916
where the time goes:
time: 588 us; the launch traced here: 589 us
  blocking collectives  191 us (32%)
  matrix products  160 us (27%)
  waiting for transfers between devices  151 us (26%)
  local copies, waits for them, and re-layouts  48.8 us (8%)
  other arithmetic  30.1 us (5%)
  starting transfers between devices  7.84 us (1%)
    all_to_all x1, blocking collectives, shards(): lax.all_to_all(outgoing, ('px', 'py'), split_axis=1, concat_axis=0, tiled...  191 us
    all_to_all x1, waiting for transfers between devices, shards(): lax.all_to_all(sent, ('px', 'py'), split_axis=0, concat_axis=1, tiled=True)  151 us
    dot_general x1, matrix products, shards(): spectral = jnp.einsum('kxb,ab->kxa', spectral, table_y, precision=high)  44.8 us
    dot_general x1, matrix products, shards(): spectral = jnp.einsum('ax,kxy->kay', table_x, planes, precision=high)  30.5 us
    dot_general x1, matrix products, shards(): returned = jnp.einsum('ax,kay->kxy', table_x, returned, precision=high)  29.6 us
    dot_general x1, matrix products, shards(): returned = jnp.einsum('kxa,ab->kxb', scaled, table_y, precision=high)  22.3 us
    dot_general x1, matrix products, shards(): return jnp.einsum('kxy,zk->xyz', gathered, modes, precision=high)  21.9 us
    dot_general x1, other arithmetic, shards(): spectral = jnp.einsum('ax,kxy->kay', table_x, planes, precision=high)  15 us
  transfers between devices with their start and end apart: 1, of which 1 were waited for; matrix products, arithmetic and copies ran while one was open for 5% of the time, Pallas kernels for 0%

commit v1 on v0

v1 whole, which is shorter than its diff:
```python
import jax
import jax.numpy as jnp
import numpy as np
from jax import lax
from jax.sharding import PartitionSpec as P

HIGH = lax.Precision.HIGH


def cosine_table(length):
    rows = np.arange(length, dtype=np.float64)[:, None]
    cols = np.arange(length, dtype=np.float64)[None, :]
    scale = np.where(rows == 0.0, np.sqrt(1.0 / length), np.sqrt(2.0 / length))
    return scale * np.cos(np.pi * (cols + 0.5) * rows / length)


def laplace_eigen(length):
    return 4.0 * np.sin(0.5 * np.pi * np.arange(length, dtype=np.float64) / length) ** 2


def sine_table(count):
    m = np.arange(1, count + 1, dtype=np.float64)
    table = np.sqrt(2.0 / (count + 1)) * np.sin(np.pi * np.outer(m, m) / (count + 1))
    return table, np.cos(np.pi * m / (count + 1))


def f32(table):
    return jnp.asarray(np.asarray(table, dtype=np.float32))


def mul(spec, *arrays):
    return jnp.einsum(spec, *arrays, precision=HIGH, preferred_element_type=jnp.float32)


def edges(table):
    return np.stack([table[:, 0], table[:, -1]])


def interfaces(xe, ye, eigen, bx, by):
    count_x, count_y = xe.shape[:2]
    cx, cy = cosine_table(bx), cosine_table(by)
    ex, ey = edges(cx), edges(cy)
    mu, nu = laplace_eigen(bx), laplace_eigen(by)
    nu_all = laplace_eigen(by * count_y)
    whole = cosine_table(by * count_y).reshape(by * count_y, count_y, by)
    turn = f32(np.einsum("bjy,qy->bjq", whole, cy))
    inverse = 1.0 / (eigen[:, None, None] + f32(mu[:, None] + nu[None, :]))
    inverse_all = 1.0 / (eigen[:, None, None] + f32(mu[:, None] + nu_all[None, :]))
    ex32, ey32 = f32(ex), f32(ey)
    sin_x, cos_x = (f32(t) for t in sine_table(count_x - 1))
    sin_y, cos_y = (f32(t) for t in sine_table(count_y - 1))

    own_y = jnp.sum(inverse * f32(ey[0] * ey[0]), -1)
    far_y = jnp.sum(inverse * f32(ey[0] * ey[1]), -1)
    gain_y = 1.0 / (1.0 + 2.0 * own_y[:, None] - 2.0 * far_y[:, None] * cos_y[None, :, None])
    own_x = jnp.sum(inverse_all * f32(ex[0] * ex[0])[:, None], 1)
    far_x = jnp.sum(inverse_all * f32(ex[0] * ex[1])[:, None], 1)
    gain_x = 1.0 / (1.0 + 2.0 * own_x[:, None] - 2.0 * far_x[:, None] * cos_x[None, :, None])

    def solve_y(values):
        jump = values[:, 1:, :, 0] - values[:, :-1, :, 1]
        modal = mul("ml,ilnp->imnp", sin_y, jump) * gain_y.transpose(1, 0, 2)
        return mul("ml,ilnp->imnp", sin_y, modal)

    def loads_y(w):
        first = jnp.pad(w, ((0, 0), (1, 0), (0, 0), (0, 0)))
        last = jnp.pad(w, ((0, 0), (0, 1), (0, 0), (0, 0)))
        return jnp.stack([first, -last], 3)

    def loads_x(w):
        first = jnp.pad(w, ((1, 0), (0, 0), (0, 0), (0, 0)))
        last = jnp.pad(w, ((0, 1), (0, 0), (0, 0), (0, 0)))
        return jnp.stack([first, -last], 3)

    wy = solve_y(ye)
    load = loads_y(wy)
    weighted = load[:, :, :, None] * ex32[:, None, :]
    moved = mul("ijnfep,npq->ijnfeq", weighted, inverse)
    xs = xe - jnp.sum(moved * ey32, 4)
    jump = xs[1:, :, :, 0] - xs[:-1, :, :, 1]
    spectral = mul("ijnq,bjq->inb", jump, turn)
    spectral = mul("ml,lnb->mnb", sin_x, spectral) * gain_x.transpose(1, 0, 2)
    spectral = mul("ml,lnb->mnb", sin_x, spectral)
    wx = mul("inb,bjq->ijnq", spectral, turn)
    xload = loads_x(wx)
    weighted = xload[:, :, :, None] * ey32[:, None, :]
    moved = mul("ijnfeq,npq->ijnfep", weighted, inverse)
    wy = wy - solve_y(jnp.sum(moved * ex32, 4))
    return xload, loads_y(wy)


def shards(source, layer_mass, modes, mode_eigen):
    bx, by, levels = source.shape
    count_x = lax.axis_size("px")
    count_y = lax.axis_size("py")
    devices = count_x * count_y
    group = levels // devices
    cx, cy = cosine_table(bx), cosine_table(by)
    mu, nu = laplace_eigen(bx), laplace_eigen(by)
    cx32, cy32, ex, ey = f32(cx), f32(cy), f32(edges(cx)), f32(edges(cy))

    field = mul("xyz,zk->xyk", source, layer_mass[:, None] * modes)
    field = mul("qy,xyk->xqk", cy32, field)
    field = mul("px,xqk->pqk", cx32, field)
    inverse = 1.0 / (mode_eigen + f32(mu[:, None] + nu[None, :])[:, :, None])
    local = field * inverse
    xe = jnp.stack([jnp.sum(local * e[:, None, None], 0) for e in ex])
    ye = jnp.stack([jnp.sum(local * e[:, None], 1) for e in ey])

    packed = jnp.concatenate([xe.reshape(2 * by, levels), ye.reshape(2 * bx, levels)]).T
    sent = packed.reshape(devices, group, 2 * (bx + by))
    got = lax.all_to_all(sent, ("px", "py"), split_axis=0, concat_axis=0, tiled=True)
    got = got.reshape(count_x, count_y, group, 2 * (bx + by))
    first_mode = (lax.axis_index("px") * count_y + lax.axis_index("py")) * group
    eigen = lax.dynamic_slice_in_dim(mode_eigen, first_mode, group)
    xl, yl = interfaces(
        got[..., : 2 * by].reshape(count_x, count_y, group, 2, by),
        got[..., 2 * by :].reshape(count_x, count_y, group, 2, bx),
        eigen,
        bx,
        by,
    )
    back = jnp.concatenate(
        [xl.reshape(devices, group, 2 * by), yl.reshape(devices, group, 2 * bx)], 2
    )
    back = lax.all_to_all(back, ("px", "py"), split_axis=0, concat_axis=0, tiled=True)
    back = back.reshape(levels, 2 * (bx + by)).T
    xl = back[: 2 * by].reshape(2, by, levels)
    yl = back[2 * by :].reshape(2, bx, levels)

    load = ex[0][:, None, None] * xl[0] + ex[1][:, None, None] * xl[1]
    load = load + ey[0][:, None] * yl[0][:, None] + ey[1][:, None] * yl[1][:, None]
    local = local - load * inverse
    local = mul("px,pqk->xqk", cx32, local)
    local = mul("qy,xqk->xyk", cy32, local)
    return mul("xyk,zk->xyz", local, modes)


def solution(mesh):
    placed = (P("px", "py", None), P(), P(), P())
    return jax.shard_map(
        shards, mesh=mesh, in_specs=placed, out_specs=P("px", "py", None), check_vma=False
    )
```

time: 588 us -> 103 us (0.18)
  blocking collectives: 191 us -> 12.7 us
  waiting for transfers between devices: 151 us -> 9.16 us
  matrix products: 160 us -> 59.6 us
  local copies, waits for them, and re-layouts: 48.8 us -> 12 us
  other arithmetic: 30.1 us -> 1.12 us
    all_to_all x1, blocking collectives: 191 us -> 12.7 us  [shards(): lax.all_to_all(back, ('px', 'py'), split_axis=0, concat_axis=0, tiled=True)]
    all_to_all x1, waiting for transfers between devices: 151 us -> 9.16 us  [shards(): lax.all_to_all(sent, ('px', 'py'), split_axis=0, concat_axis=0, tiled=True)]
    dot_general x6 -> x16, matrix products: 160 us -> 59.6 us  [mul(): jnp.einsum(spec, *arrays, precision=HIGH, preferred_element_type=jnp.floa...]
    reshape x5 -> x8, local copies, waits for them, and re-layouts: 42.4 us -> 1.46 us  [the longest x1 0.77 us: shards(): sent = packed.reshape(devices, group, 2 * (bx + by))]
    dot_general x2 -> x0, other arithmetic: 29.9 us -> none  [the longest x1 15 us: shards(): spectral = jnp.einsum('ax,kxy->kay', table_x, planes, precision=high)]
    transpose x0 -> x1, local copies, waits for them, and re-layouts: none -> 9.42 us  [mul(): jnp.einsum(spec, *arrays, precision=HIGH, preferred_element_type=jnp.floa...]
    unnamed x7 -> x32, local copies, waits for them, and re-layouts: 6.32 us -> 0.09 us
  transfers between devices with their start and end apart: 1 -> 1, of which waited for: 1 -> 1; matrix products, arithmetic and copies ran while one was open for 5% -> 1% of each run, Pallas kernels for 0% -> 0%
where the time goes in v1:
time: 103 us
  matrix products  59.6 us (58%)
  blocking collectives  12.7 us (12%)
  local copies, waits for them, and re-layouts  12 us (12%)
  waiting for transfers between devices  9.16 us (9%)
  starting transfers between devices  7.51 us (7%)
  other arithmetic  1.12 us (1%)
    dot_general x16, matrix products, mul(): jnp.einsum(spec, *arrays, precision=HIGH, preferred_element_type=jnp.floa...  59.6 us
    all_to_all x1, blocking collectives, shards(): lax.all_to_all(back, ('px', 'py'), split_axis=0, concat_axis=0, tiled=True)  12.7 us
    transpose x1, local copies, waits for them, and re-layouts, mul(): jnp.einsum(spec, *arrays, precision=HIGH, preferred_element_type=jnp.floa...  9.42 us
    all_to_all x1, waiting for transfers between devices, shards(): lax.all_to_all(sent, ('px', 'py'), split_axis=0, concat_axis=0, tiled=True)  9.16 us
    all_to_all x1, starting transfers between devices, shards(): lax.all_to_all(sent, ('px', 'py'), split_axis=0, concat_axis=0, tiled=True)  7.51 us
  transfers between devices with their start and end apart: 1, of which 1 were waited for; matrix products, arithmetic and copies ran while one was open for 1% of the time, Pallas kernels for 0%

profile of v1, /device:TPU:0, one launch (start us, length us, event | category | flops | bytes accessed | tf_op | source)
XLA Modules:
  0.0 102.6 jit_solution(17754532792456202456)
XLA Ops:
  0.0 6.6 %convolution_bitcast_fusion = f32[128,128,128]{1,2,0:T(8,128)S(1)} fusion(f32[128,128,128]{2,1,0:T(8,128)} %param.22, f32[128,128]{1,0:T(8,128)} %param.24, f32[128]{0:T(128)} %param.23), kind=kOutput, calls=%fused_computation.34 | convolution fusion | flops 1610629120 | bytes 16843264 | tf_op jit(solution)/shard_map/xyz,zk->xyk/dot_general | solution.py:32
  6.6 10.6 %fusion.28 = f32[128,128,128]{1,0,2:T(8,128)} fusion(f32[128,128,1]{1,0,2:T(8,128)S(1)} %copy-done.2, f32[128,128,128]{1,2,0:T(8,128)S(1)} %convolution_bitcast_fusion), kind=kOutput, calls=%fused_computation.33 | convolution fusion | flops 1610612736 | bytes 16842752 | tf_op jit(solution)/shard_map/qy,xyk->xqk/dot_general | solution.py:32
  17.2 9.4 %copy.84 = f32[128,128,128]{2,0,1:T(8,128)} copy(f32[128,128,128]{1,0,2:T(8,128)} %fusion.28) | data formatting | bytes 16777216 | tf_op jit(solution)/shard_map/qy,xyk->xqk/transpose | solution.py:32
  26.7 10.8 %multiply_reduce_fusion.3 = (f32[128,128]{1,0:T(8,128)S(1)}, f32[128,128]{1,0:T(8,128)S(1)}, f32[128,128]{1,0:T(8,128)S(1)}, f32[128,128]{1,0:T(8,128)S(1)}, f32[128,128,128]{2,0,1:T(8,128)}) fusion(f32[128]{0:T(128)S(1)} %copy-done.13, f32[128]{0:T(128)S(1)} %copy-done.14, f32[128,128]{0,1:T(8,128)S(1)} %copy-done.11, f32[128]{0:T(128)S(1)} %copy-done.10, ...), kind=kOutput, calls=%fused_computation.19 | convolution fusion | flops 1633615872 | bytes 17171968 | tf_op jit(solution)/shard_map/px,xqk->pqk/dot_general | solution.py:32
  37.8 0.8 reshape.89
  38.5 7.5 %all-to-all-start = ((f32[32,4,512]{2,1,0:T(4,128)}), f32[32,4,512]{2,1,0:T(4,128)S(1)}, u32[]{:S(2)}, u32[]{:S(2)}) async-start(f32[32,4,512]{2,1,0:T(4,128)} %reshape.89), calls=%async_computation | async-start | bytes 524288 | tf_op jit(solution)/shard_map/all_to_all | solution.py:112
  46.1 0.3 multiply_reduce_fusion.7
  46.5 0.4 multiply_reduce_fusion.5
  46.9 9.2 %all-to-all-done = f32[32,4,512]{2,1,0:T(4,128)S(1)} async-done(((f32[32,4,512]{2,1,0:T(4,128)}), f32[32,4,512]{2,1,0:T(4,128)S(1)}, u32[]{:S(2)}, u32[]{:S(2)}) %all-to-all-start) | async-done | bytes 262176 | tf_op jit(solution)/shard_map/all_to_all | solution.py:112
  56.4 0.2 fusion.37
  56.6 0.2 convolution_bitcast_fusion.8
  57.0 0.3 fusion.33
  57.5 0.6 convolution_bitcast_fusion.7
  58.1 0.2 convolution_multiply_fusion
  58.3 0.2 convolution_bitcast_fusion.6
  58.4 0.4 convolution_bitcast_fusion.5
  58.9 0.5 fusion.34
  59.4 0.2 fusion.36
  59.6 0.2 fusion.35
  60.4 0.2 copy.99
  60.5 12.7 %all_to_all.10 = f32[32,4,512]{2,1,0:T(4,128)S(1)} all-to-all(f32[32,4,512]{2,1,0:T(4,128)S(1)} %copy.99), channel_id=1, replica_groups=mesh['px'=8,'py'=4] {'px','py'}, dimensions={0} | all-to-all | bytes 524288 | tf_op jit(solution)/shard_map/all_to_all | solution.py:126
  73.8 9.6 %fusion.6 = f32[128,128,128]{2,0,1:T(8,128)S(1)} fusion(f32[128,128,1]{1,0,2:T(8,128)S(1)} %copy-done.2, f32[128,128,128]{2,0,1:T(8,128)} %get-tuple-element.29, f32[128,128]{1,0:T(8,128)S(1)} %copy.103, f32[128,128]{1,0:T(8,128)S(1)} %copy.102, f32[128,128]{1,0:T(8,128)S(1)} %copy.101, f32[128,128]{1,0:T(8,128)S(1)} %copy.100, f32[128]{0:T(128)S(1)} %copy-done.14, ...), kind=kOutput, calls=%fused_computation.6 | convolution fusion | flops 1633681408 | bytes 17171968 | tf_op jit(solution)/shard_map/px,pqk->xqk/dot_general | solution.py:32
  83.4 9.9 %fusion.2 = f32[128,128,128]{2,1,0:T(8,128)S(1)} fusion(f32[128,128,1]{1,0,2:T(8,128)S(1)} %copy-done.2, f32[128,128,128]{2,0,1:T(8,128)S(1)} %fusion.6), kind=kOutput, calls=%fused_computation.2 | convolution fusion | flops 1610612736 | bytes 16842752 | tf_op jit(solution)/shard_map/qy,xqk->xyk/dot_general | solution.py:32
  93.3 9.3 %fusion = f32[128,128,128]{2,1,0:T(8,128)} fusion(f32[128,128,128]{2,1,0:T(8,128)S(1)} %fusion.2, f32[128,128]{1,0:T(8,128)S(1)} %copy-done.1), kind=kOutput, calls=%fused_computation | convolution fusion | flops 1610612736 | bytes 16842752 | tf_op jit(solution)/shard_map/xyk,zk->xyz/dot_general | solution.py:32
  (66 shorter events, 2.0 us)
Async XLA Ops:
  0.0 6.6 %copy-start.2 = (f32[128,128,1]{1,0,2:T(8,128)S(1)}, f32[128,128,1]{1,0,2:T(8,128)}, u32[]{:S(2)}) copy-start(f32[128,128,1]{1,0,2:T(8,128)} %constant.78) | copy-start | bytes 196612
  17.2 9.4 %copy-start.10 = (f32[128]{0:T(128)S(1)}, f32[128]{0:T(128)}, u32[]{:S(2)}) copy-start(f32[128]{0:T(128)} %param.25) | copy-start | bytes 1540
  17.2 9.4 %copy-start.11 = (f32[128,128]{0,1:T(8,128)S(1)}, f32[128,128]{0,1:T(8,128)}, u32[]{:S(2)}) copy-start(f32[128,128]{0,1:T(8,128)} %constant.19.clone) | copy-start | bytes 196612
  17.2 9.4 %copy-start.13 = (f32[128]{0:T(128)S(1)}, f32[128]{0:T(128)}, u32[]{:S(2)}) copy-start(f32[128]{0:T(128)} %constant.75) | copy-start | bytes 1540
  17.2 9.4 %copy-start.14 = (f32[128]{0:T(128)S(1)}, f32[128]{0:T(128)}, u32[]{:S(2)}) copy-start(f32[128]{0:T(128)} %constant.77) | copy-start | bytes 1540
  26.6 19.5 %copy-start.4 = (f32[128,128]{1,0:T(8,128)S(1)}, f32[128,128]{1,0:T(8,128)}, u32[]{:S(2)}) copy-start(f32[128,128]{1,0:T(8,128)} %constant.80) | copy-start | bytes 196612
  26.6 19.5 %copy-start.7 = (f32[128]{0:T(128)S(1)}, f32[128]{0:T(128)}, u32[]{:S(2)}) copy-start(f32[128]{0:T(128)} %constant.60.clone) | copy-start | bytes 1540
  26.6 19.5 %copy-start.8 = (f32[128]{0:T(128)S(1)}, f32[128]{0:T(128)}, u32[]{:S(2)}) copy-start(f32[128]{0:T(128)} %constant.61.clone) | copy-start | bytes 1540
  26.7 19.8 %copy-start.9 = (f32[3]{0:T(128)S(1)}, f32[3]{0:T(128)}, u32[]{:S(2)}) copy-start(f32[3]{0:T(128)} %constant.59.clone) | copy-start | bytes 40
  26.7 19.9 %copy-start.3 = (f32[128,512]{1,0:T(8,128)S(1)}, f32[128,512]{1,0:T(8,128)}, u32[]{:S(2)}) copy-start(f32[128,512]{1,0:T(8,128)} %constant.55.clone) | copy-start | bytes 786436
  26.7 29.7 %copy-start.5 = (f32[3,3,1,1]{1,0,3,2:T(4,128)S(1)}, f32[3,3,1,1]{1,0,3,2:T(4,128)}, u32[]{:S(2)}) copy-start(f32[3,3,1,1]{1,0,3,2:T(4,128)} %constant.81) | copy-start | bytes 112
  26.7 30.3 %copy-start.12 = (f32[2,128]{1,0:T(2,128)S(1)}, f32[2,128]{1,0:T(2,128)}, u32[]{:S(2)}) copy-start(f32[2,128]{1,0:T(2,128)} %constant.18.clone) | copy-start | bytes 3076
  26.7 30.8 %copy-start = (f32[512,4,128,1]{2,0,1,3:T(8,128)S(1)}, f32[512,4,128,1]{2,0,1,3:T(8,128)}, u32[]{:S(2)}) copy-start(f32[512,4,128,1]{2,0,1,3:T(8,128)} %constant.82) | copy-start | bytes 3145732
  26.7 31.4 %copy-start.6 = (f32[7,7,1]{1,0,2:T(8,128)S(1)}, f32[7,7,1]{1,0,2:T(8,128)}, u32[]{:S(2)}) copy-start(f32[7,7,1]{1,0,2:T(8,128)} %constant.79) | copy-start | bytes 592
  26.7 31.4 %copy-start.15 = (f32[7]{0:T(128)S(1)}, f32[7]{0:T(128)}, u32[]{:S(2)}) copy-start(f32[7]{0:T(128)} %constant.57.clone) | copy-start | bytes 88
  38.5 17.6 %all-to-all-start = ((f32[32,4,512]{2,1,0:T(4,128)}), f32[32,4,512]{2,1,0:T(4,128)S(1)}, u32[]{:S(2)}, u32[]{:S(2)}) async-start(f32[32,4,512]{2,1,0:T(4,128)} %reshape.89), calls=%async_computation | async-start | bytes 524288 | tf_op jit(solution)/shard_map/all_to_all | solution.py:112
  83.4 9.9 %copy-start.1 = (f32[128,128]{1,0:T(8,128)S(1)}, f32[128,128]{1,0:T(8,128)}, u32[]{:S(2)}) copy-start(f32[128,128]{1,0:T(8,128)} %param.24) | copy-start | bytes 196612

commit v2 on v1

--- a/solution.py
+++ b/solution.py
@@ -1,7 +1,11 @@
+import functools
+
 import jax
 import jax.numpy as jnp
 import numpy as np
 from jax import lax
+from jax.experimental import pallas as pl
+from jax.experimental.pallas import tpu as pltpu
 from jax.sharding import PartitionSpec as P
 
 HIGH = lax.Precision.HIGH
@@ -89,6 +93,215 @@
     return xload, loads_y(wy)
 
 
+BF16 = jnp.bfloat16
+F32 = jnp.float32
+
+
+def split(values):
+    high = values.astype(BF16)
+    return high, (values - high.astype(F32)).astype(BF16)
+
+
+def left_table(table):
+    table = np.asarray(table, dtype=np.float32)
+    high = table.astype(BF16)
+    low = (table - high.astype(np.float32)).astype(BF16)
+    return jnp.asarray(np.concatenate([high, high, low], 1))
+
+
+def stack_rows(values):
+    high, low = split(values)
+    return jnp.concatenate([high, low, high], 0)
+
+
+def times_right(values, factor):
+    high, low = split(values)
+    fhigh, flow = split(factor)
+    return jnp.dot(
+        jnp.concatenate([high, low, high], 1),
+        jnp.concatenate([fhigh, fhigh, flow], 0),
+        preferred_element_type=F32,
+    )
+
+
+def times_left(table, values):
+    return jnp.dot(table, stack_rows(values), preferred_element_type=F32)
+
+
+def forward_kernel(
+    steps_x, xb, qb, nu_ref, ey_ref, source_ref, mass_ref, modes_ref, cx_ref, cy_ref, ex_ref,
+    mu_ref, eigen_ref, local_ref, edges_ref, half_ref, even_ref, odd_ref, xe_ref,
+):
+    step = pl.program_id(0)
+    by, levels = source_ref.shape[1:]
+    bx = mu_ref.shape[0]
+
+    @pl.when(step < steps_x)
+    def _():
+        field = times_right(
+            source_ref[...].reshape(xb * by, levels) * mass_ref[...], modes_ref[...]
+        )
+        for x in range(0, xb, 2):
+            pair = jnp.concatenate(
+                [field[x * by : (x + 1) * by], field[(x + 1) * by : (x + 2) * by]], 1
+            )
+            pair = times_left(cy_ref[...], pair)
+            row = pl.multiple_of((step * xb + x) * by, 2 * by)
+            half_ref[pl.ds(row, by)] = pair[:, :levels]
+            half_ref[pl.ds(row + by, by)] = pair[:, levels:]
+
+    @pl.when(step == steps_x)
+    def _():
+        even_ref[...] = jnp.zeros_like(even_ref)
+        odd_ref[...] = jnp.zeros_like(odd_ref)
+
+    @pl.when(step >= steps_x)
+    def _():
+        first = (step - steps_x) * qb
+        columns = jnp.concatenate(
+            [half_ref[pl.ds(first + q, bx, stride=by), :] for q in range(qb)], 1
+        )
+        spectral = times_left(cx_ref[...], columns)
+        base = mu_ref[...] + eigen_ref[...]
+        weight = ex_ref[...]
+        sums = [None, None]
+        sign = jnp.where(
+            lax.broadcasted_iota(jnp.int32, (8, levels), 0) % 2 == 0, 1.0, -1.0
+        ).astype(F32)
+        rows = [[], []]
+        for q in range(qb):
+            value = spectral[:, q * levels : (q + 1) * levels] / (base + nu_ref[first + q])
+            local_ref[q] = value
+            folded = jnp.sum((value * weight).reshape(bx // 8, 8, levels), 0)
+            rows[0].append(jnp.sum(folded, 0, keepdims=True))
+            rows[1].append(jnp.sum(folded * sign, 0, keepdims=True))
+            term = value * ey_ref[first + q]
+            sums[q % 2] = term if sums[q % 2] is None else sums[q % 2] + term
+        even_ref[...] += sums[0]
+        odd_ref[...] += sums[1]
+        here = pl.ds(pl.multiple_of(first, qb), qb)
+        xe_ref[0, here] = jnp.concatenate(rows[0], 0)
+        xe_ref[1, here] = jnp.concatenate(rows[1], 0)
+
+    @pl.when(step == pl.num_programs(0) - 1)
+    def _():
+        even, odd = even_ref[...], odd_ref[...]
+        edges_ref[:, : 2 * by] = xe_ref[...].reshape(2 * by, levels).T
+        edges_ref[:, 2 * by :] = jnp.concatenate([even + odd, even - odd], 0).T
+
+
+def backward_kernel(
+    steps_q, xb, qb, nu_ref, ey_ref, local_ref, modes_ref, cx_ref, cy_ref, ex_ref, mu_ref,
+    eigen_ref, loads_ref, out_ref, half_ref, xl_ref, yl_ref, turned_ref,
+):
+    step = pl.program_id(0)
+    bx, levels = mu_ref.shape
+    by = xl_ref.shape[1]
+
+    @pl.when(step == 0)
+    def _():
+        xl_ref[...] = loads_ref[:, : 2 * by].T.reshape(2, by, levels)
+        yl_ref[...] = loads_ref[:, 2 * by :].T.reshape(2, bx, levels)
+        turned_ref[...] = modes_ref[...].T
+
+    @pl.when(step < steps_q)
+    def _():
+        first = step * qb
+        base = mu_ref[...] + eigen_ref[...]
+        weight = ex_ref[...]
+        flip = jnp.where(
+            lax.broadcasted_iota(jnp.int32, (bx, levels), 0) % 2 == 0, weight, -weight
+        )
+        here = pl.ds(pl.multiple_of(first, qb), qb)
+        left, right = xl_ref[0, here], xl_ref[1, here]
+        both = [yl_ref[0] + yl_ref[1], yl_ref[0] - yl_ref[1]]
+        columns = []
+        for q in range(qb):
+            load = weight * left[q : q + 1] + flip * right[q : q + 1]
+            load = load + ey_ref[first + q] * both[q % 2]
+            columns.append(local_ref[q] - load / (base + nu_ref[first + q]))
+        field = times_left(cx_ref[...], jnp.concatenate(columns, 1))
+        for q in range(qb):
+            half_ref[pl.ds(first + q, bx, stride=by), :] = field[:, q * levels : (q + 1) * levels]
+
+    @pl.when(step >= steps_q)
+    def _():
+        parts = []
+        for x in range(0, xb, 2):
+            row = pl.multiple_of(((step - steps_q) * xb + x) * by, 2 * by)
+            pair = jnp.concatenate([half_ref[pl.ds(row, by)], half_ref[pl.ds(row + by, by)]], 1)
+            pair = times_left(cy_ref[...], pair)
+            parts += [pair[:, :levels], pair[:, levels:]]
+        field = jnp.concatenate(parts, 0)
+        out_ref[...] = times_right(field, turned_ref[...]).reshape(xb, by, levels)
+
+
+def whole_block(array):
+    return pl.BlockSpec(array.shape, lambda i: (0,) * array.ndim)
+
+
+SCALARS = pl.BlockSpec(memory_space=pltpu.SMEM)
+VMEM_LIMIT = 56 * 1024 * 1024
+
+
+def forward(source, mass, modes, cx, cy, ex, mu, eigen, nu, ey):
+    bx, by, levels = source.shape
+    xb, qb = min(32, bx), min(16, by)
+    steps_x, steps_q = bx // xb, by // qb
+    return pl.pallas_call(
+        functools.partial(forward_kernel, steps_x, xb, qb),
+        name="forward",
+        grid=(steps_x + steps_q,),
+        in_specs=[
+            SCALARS,
+            SCALARS,
+            pl.BlockSpec((xb, by, levels), lambda i: (jnp.minimum(i, steps_x - 1), 0, 0)),
+        ]
+        + [whole_block(a) for a in (mass, modes, cx, cy, ex, mu, eigen)],
+        out_specs=[
+            pl.BlockSpec((qb, bx, levels), lambda i: (jnp.maximum(i - steps_x, 0), 0, 0)),
+            pl.BlockSpec((levels, 2 * (bx + by)), lambda i: (0, 0)),
+        ],
+        out_shape=[
+            jax.ShapeDtypeStruct((by, bx, levels), F32),
+            jax.ShapeDtypeStruct((levels, 2 * (bx + by)), F32),
+        ],
+        scratch_shapes=[
+            pltpu.VMEM((bx * by, levels), F32),
+            pltpu.VMEM((bx, levels), F32),
+            pltpu.VMEM((bx, levels), F32),
+            pltpu.VMEM((2, by, levels), F32),
+        ],
+        compiler_params=pltpu.CompilerParams(vmem_limit_bytes=VMEM_LIMIT),
+    )(nu, ey, source, mass, modes, cx, cy, ex, mu, eigen)
+
+
+def backward(local, modes, cx, cy, ex, mu, eigen, nu, ey, loads):
+    by, bx, levels = local.shape
+    xb, qb = min(32, bx), min(16, by)
+    steps_x, steps_q = bx // xb, by // qb
+    return pl.pallas_call(
+        functools.partial(backward_kernel, steps_q, xb, qb),
+        name="backward",
+        grid=(steps_x + steps_q,),
+        in_specs=[
+            SCALARS,
+            SCALARS,
+            pl.BlockSpec((qb, bx, levels), lambda i: (jnp.minimum(i, steps_q - 1), 0, 0)),
+        ]
+        + [whole_block(a) for a in (modes, cx, cy, ex, mu, eigen, loads)],
+        out_specs=pl.BlockSpec((xb, by, levels), lambda i: (jnp.maximum(i - steps_q, 0), 0, 0)),
+        out_shape=jax.ShapeDtypeStruct((bx, by, levels), F32),
+        scratch_shapes=[
+            pltpu.VMEM((bx * by, levels), F32),
+            pltpu.VMEM((2, by, levels), F32),
+            pltpu.VMEM((2, bx, levels), F32),
+            pltpu.VMEM((levels, levels), F32),
+        ],
+        compiler_params=pltpu.CompilerParams(vmem_limit_bytes=VMEM_LIMIT),
+    )(nu, ey, local, modes, cx, cy, ex, mu, eigen, loads)
+
+
 def shards(source, layer_mass, modes, mode_eigen):
     bx, by, levels = source.shape
     count_x = lax.axis_size("px")
@@ -97,17 +310,15 @@
     group = levels // devices
     cx, cy = cosine_table(bx), cosine_table(by)
     mu, nu = laplace_eigen(bx), laplace_eigen(by)
-    cx32, cy32, ex, ey = f32(cx), f32(cy), f32(edges(cx)), f32(edges(cy))
-
-    field = mul("xyz,zk->xyk", source, layer_mass[:, None] * modes)
-    field = mul("qy,xyk->xqk", cy32, field)
-    field = mul("px,xqk->pqk", cx32, field)
-    inverse = 1.0 / (mode_eigen + f32(mu[:, None] + nu[None, :])[:, :, None])
-    local = field * inverse
-    xe = jnp.stack([jnp.sum(local * e[:, None, None], 0) for e in ex])
-    ye = jnp.stack([jnp.sum(local * e[:, None], 1) for e in ey])
-
-    packed = jnp.concatenate([xe.reshape(2 * by, levels), ye.reshape(2 * bx, levels)]).T
+    nu32, ey32 = f32(nu), f32(cy[:, 0])
+    ex = f32(np.repeat(cx[:, :1], levels, 1))
+    mu32 = f32(np.repeat(mu[:, None], levels, 1))
+    eigen_row = mode_eigen.reshape(1, levels)
+
+    local, packed = forward(
+        source, layer_mass.reshape(1, levels), modes, left_table(cx), left_table(cy), ex, mu32,
+        eigen_row, nu32, ey32,
+    )
     sent = packed.reshape(devices, group, 2 * (bx + by))
     got = lax.all_to_all(sent, ("px", "py"), split_axis=0, concat_axis=0, tiled=True)
     got = got.reshape(count_x, count_y, group, 2 * (bx + by))
@@ -124,16 +335,10 @@
         [xl.reshape(devices, group, 2 * by), yl.reshape(devices, group, 2 * bx)], 2
     )
     back = lax.all_to_all(back, ("px", "py"), split_axis=0, concat_axis=0, tiled=True)
-    back = back.reshape(levels, 2 * (bx + by)).T
-    xl = back[: 2 * by].reshape(2, by, levels)
-    yl = back[2 * by :].reshape(2, bx, levels)
-
-    load = ex[0][:, None, None] * xl[0] + ex[1][:, None, None] * xl[1]
-    load = load + ey[0][:, None] * yl[0][:, None] + ey[1][:, None] * yl[1][:, None]
-    local = local - load * inverse
-    local = mul("px,pqk->xqk", cx32, local)
-    local = mul("qy,xqk->xyk", cy32, local)
-    return mul("xyk,zk->xyz", local, modes)
+    return backward(
+        local, modes, left_table(cx.T), left_table(cy.T), ex, mu32, eigen_row, nu32, ey32,
+        back.reshape(levels, 2 * (bx + by)),
+    )
 
 
 def solution(mesh):

time: 103 us -> 75.5 us (0.73)
  matrix products: 59.6 us -> 2.88 us
  Pallas kernels: 0 us -> 37.8 us
  local copies, waits for them, and re-layouts: 12 us -> 3.63 us
    dot_general x16 -> x10, matrix products: 59.6 us -> 2.88 us  [mul(): jnp.einsum(spec, *arrays, precision=HIGH, preferred_element_type=jnp.floa...]
    pallas_call x0 -> x2, Pallas kernels: none -> 37.8 us  [the longest x1 19.1 us: backward(): pl.pallas_call(functools.partial(backward_kernel, steps_q, xb, qb), name=...]
    transpose x1 -> x0, local copies, waits for them, and re-layouts: 9.42 us -> none  [mul(): jnp.einsum(spec, *arrays, precision=HIGH, preferred_element_type=jnp.floa...]
where the time goes in v2:
time: 75.5 us; the launch traced here: 75.1 us
  Pallas kernels  37.8 us (50%)
  blocking collectives  12.7 us (17%)
  waiting for transfers between devices  9.33 us (12%)
  starting transfers between devices  7.34 us (10%)
  local copies, waits for them, and re-layouts  3.63 us (5%)
  matrix products  2.88 us (4%)
  other arithmetic  1.08 us (1%)
    pallas_call x1, Pallas kernels, backward(): pl.pallas_call(functools.partial(backward_kernel, steps_q, xb, qb), name=...  19.1 us
    pallas_call x1, Pallas kernels, forward(): pl.pallas_call(functools.partial(forward_kernel, steps_x, xb, qb), name='...  18.6 us
    all_to_all x1, blocking collectives, shards(): lax.all_to_all(back, ('px', 'py'), split_axis=0, concat_axis=0, tiled=True)  12.7 us
    all_to_all x1, waiting for transfers between devices, shards(): lax.all_to_all(sent, ('px', 'py'), split_axis=0, concat_axis=0, tiled=True)  9.33 us
    all_to_all x1, starting transfers between devices, shards(): lax.all_to_all(sent, ('px', 'py'), split_axis=0, concat_axis=0, tiled=True)  7.34 us
    dot_general x10, matrix products, mul(): jnp.einsum(spec, *arrays, precision=HIGH, preferred_element_type=jnp.floa...  2.88 us
    reshape x1, local copies, waits for them, and re-layouts, shards(): sent = packed.reshape(devices, group, 2 * (bx + by))  1.75 us
  transfers between devices with their start and end apart: 1, of which 1 were waited for; matrix products, arithmetic and copies ran while one was open for 1% of the time, Pallas kernels for 0%

profile of v2, /device:TPU:0, one launch (start us, length us, event | category | flops | bytes accessed | tf_op | source)
XLA Modules:
  0.0 75.1 jit_solution(1316611663961224856)
XLA Ops:
  0.1 18.6 %forward.1 = (f32[128,128,128]{2,1,0:T(8,128)}, f32[128,512]{1,0:T(8,128)}) custom-call(f32[128]{0:T(128)} %constant.23.clone.nu_ref, f32[128]{0:T(128)} %constant.24.clone.ey_ref, f32[128,128,128]{2,1,0:T(8,128)} %source_ref.1, f32[1,128]{1,0:T(1,128)} %bitcast.88, f32[128,128]{1,0:T(8,128)} %modes_ref.3, bf16[128,384]{1,0:T(8,128)(2,1)} %constant.64.clone.cx_ref.cy_ref, ...), custom_call_target="tpu_custom_call" | custom-call | tf_op jit(solution)/shard_map/forward/pallas_call | solution.py:251
  18.7 1.7 %reshape.70 = f32[32,4,512]{2,1,0:T(4,128)} reshape(f32[128,512]{1,0:T(8,128)} %get-tuple-element.8) | data formatting | bytes 524288 | tf_op jit(solution)/shard_map/reshape | solution.py:322
  20.5 7.3 %all-to-all-start = ((f32[32,4,512]{2,1,0:T(4,128)}), f32[32,4,512]{2,1,0:T(4,128)S(1)}, u32[]{:S(2)}, u32[]{:S(2)}) async-start(f32[32,4,512]{2,1,0:T(4,128)} %reshape.70), calls=%async_computation | async-start | bytes 524288 | tf_op jit(solution)/shard_map/all_to_all | solution.py:323
  27.9 0.3 multiply_reduce_fusion.3
  28.3 0.4 multiply_reduce_fusion.1
  28.7 9.3 %all-to-all-done = f32[32,4,512]{2,1,0:T(4,128)S(1)} async-done(((f32[32,4,512]{2,1,0:T(4,128)}), f32[32,4,512]{2,1,0:T(4,128)S(1)}, u32[]{:S(2)}, u32[]{:S(2)}) %all-to-all-start) | async-done | bytes 262176 | tf_op jit(solution)/shard_map/all_to_all | solution.py:323
  38.4 0.2 fusion.6
  38.6 0.2 convolution_bitcast_fusion.7
  39.0 0.3 fusion.2
  39.4 0.6 convolution_bitcast_fusion.6
  40.0 0.2 convolution_multiply_fusion
  40.2 0.2 convolution_bitcast_fusion.5
  40.4 0.4 convolution_bitcast_fusion.4
  40.8 0.5 fusion.3
  41.3 0.1 copy.70
  41.4 0.1 reshape.74
  41.5 0.2 fusion.5
  41.7 0.2 fusion.4
  42.0 0.1 copy.73
  42.1 0.1 reshape.75
  42.3 0.2 copy.74
  42.4 12.7 %all_to_all.10 = f32[32,4,512]{2,1,0:T(4,128)S(1)} all-to-all(f32[32,4,512]{2,1,0:T(4,128)S(1)} %copy.74), channel_id=1, replica_groups=mesh['px'=8,'py'=4] {'px','py'}, dimensions={0} | all-to-all | bytes 524288 | tf_op jit(solution)/shard_map/all_to_all | solution.py:337
  55.1 0.8 %reshape.76.loads_ref = f32[128,512]{1,0:T(8,128)} reshape(f32[32,4,512]{2,1,0:T(4,128)S(1)} %all_to_all.10) | data formatting | bytes 524288 | tf_op jit(solution)/shard_map/reshape | solution.py:340
  56.0 19.1 %backward.1 = f32[128,128,128]{2,1,0:T(8,128)} custom-call(f32[128]{0:T(128)} %constant.23.clone.nu_ref, f32[128]{0:T(128)} %constant.24.clone.ey_ref, f32[128,128,128]{2,1,0:T(8,128)} %get-tuple-element.7.local_ref, f32[128,128]{1,0:T(8,128)} %modes_ref.3, bf16[128,384]{1,0:T(8,128)(2,1)} %constant.75.clone.cx_ref.cy_ref, ...), custom_call_target="tpu_custom_call" | custom-call | tf_op jit(solution)/shard_map/backward/pallas_call | solution.py:283
  (41 shorter events, 0.9 us)
Async XLA Ops:
  0.0 27.9 %copy-start.2 = (f32[128,128]{1,0:T(8,128)S(1)}, f32[128,128]{1,0:T(8,128)}, u32[]{:S(2)}) copy-start(f32[128,128]{1,0:T(8,128)} %constant.66.clone) | copy-start | bytes 196612
  0.0 27.9 %copy-start.6 = (f32[128]{0:T(128)S(1)}, f32[128]{0:T(128)}, u32[]{:S(2)}) copy-start(f32[128]{0:T(128)} %constant.74.clone) | copy-start | bytes 1540
  0.0 27.9 %copy-start.7 = (f32[128]{0:T(128)S(1)}, f32[128]{0:T(128)}, u32[]{:S(2)}) copy-start(f32[128]{0:T(128)} %constant.73.clone) | copy-start | bytes 1540
  0.0 28.2 %copy-start.8 = (f32[3]{0:T(128)S(1)}, f32[3]{0:T(128)}, u32[]{:S(2)}) copy-start(f32[3]{0:T(128)} %constant.72.clone) | copy-start | bytes 40
  0.0 28.3 %copy-start.1 = (f32[128,512]{1,0:T(8,128)S(1)}, f32[128,512]{1,0:T(8,128)}, u32[]{:S(2)}) copy-start(f32[128,512]{1,0:T(8,128)} %constant.67.clone) | copy-start | bytes 786436
  0.0 38.4 %copy-start.3 = (f32[3,3,1,1]{1,0,3,2:T(4,128)S(1)}, f32[3,3,1,1]{1,0,3,2:T(4,128)}, u32[]{:S(2)}) copy-start(f32[3,3,1,1]{1,0,3,2:T(4,128)} %constant.89) | copy-start | bytes 112
  0.0 38.9 %copy-start.9 = (f32[2,128]{1,0:T(2,128)S(1)}, f32[2,128]{1,0:T(2,128)}, u32[]{:S(2)}) copy-start(f32[2,128]{1,0:T(2,128)} %constant.68.clone) | copy-start | bytes 3076
  0.0 39.4 %copy-start = (f32[512,4,128,1]{2,0,1,3:T(8,128)S(1)}, f32[512,4,128,1]{2,0,1,3:T(8,128)}, u32[]{:S(2)}) copy-start(f32[512,4,128,1]{2,0,1,3:T(8,128)} %constant.90) | copy-start | bytes 3145732
  0.1 40.0 %copy-start.4 = (f32[7,7,1]{1,0,2:T(8,128)S(1)}, f32[7,7,1]{1,0,2:T(8,128)}, u32[]{:S(2)}) copy-start(f32[7,7,1]{1,0,2:T(8,128)} %constant.88) | copy-start | bytes 592
  0.1 40.0 %copy-start.10 = (f32[7]{0:T(128)S(1)}, f32[7]{0:T(128)}, u32[]{:S(2)}) copy-start(f32[7]{0:T(128)} %constant.70.clone) | copy-start | bytes 88
  0.1 27.7 %copy-start.5 = (f32[128]{0:T(128)S(1)}, f32[128]{0:T(128)}, u32[]{:S(2)}) copy-start(f32[128]{0:T(128)} %param.28) | copy-start | bytes 1540
  20.5 17.6 %all-to-all-start = ((f32[32,4,512]{2,1,0:T(4,128)}), f32[32,4,512]{2,1,0:T(4,128)S(1)}, u32[]{:S(2)}, u32[]{:S(2)}) async-start(f32[32,4,512]{2,1,0:T(4,128)} %reshape.70), calls=%async_computation | async-start | bytes 524288 | tf_op jit(solution)/shard_map/all_to_all | solution.py:323
